TPU v7x, 32 devices: a whole 2x2x4 slice. The times are simulated.
32 devices in a mesh: path: 4 (over y, core), fsdp: 8 (over z, x).
Axes of the slice: x: 2, y: 2, z: 4, core: 2. Of those that a mesh axis runs over, the one named last changes fastest.
Arguments:
- input_activation_matrix: bfloat16 [4, 1536, 2048], P('path', 'fsdp'), may hold values from -6 to 6
- output_sensitivity: bfloat16 [4, 1536, 2048], P('path', 'fsdp'), may hold values from -12 to 12
- trajectory_initial_parameters: bfloat16 [4, 8, 1024, 4096], P('path', None, 'fsdp'), may hold values from -6 to 6
- trajectory_gradient_average: bfloat16 [4, 8, 1024, 4096], P('path', None, 'fsdp'), may hold values from -0.19921875 to 0.19921875
- trajectory_squared_average: bfloat16 [4, 8, 1024, 4096], P('path', None, 'fsdp'), may hold values from 0.0009994507 to 0.099609375
- common_expert_parameters: float32 [8, 2, 1024, 4096], P('path', None, 'fsdp'), may hold values from -6 to 6
- outer_inertia: float32 [8, 2, 1024, 4096], P('path', None, 'fsdp'), may hold values from -0.4 to 0.4
- trajectory_membership: int32 [4, 8], replicated, may hold values from 0 to 1
- punctual_flags: int32 [4], replicated, may hold values 0 or 1
Outputs:
- refreshed_experts: float32 [8, 2, 1024, 4096], P('path', None, 'fsdp')
- refreshed_inertia: float32 [8, 2, 1024, 4096], P('path', None, 'fsdp')
- returned: bfloat16 [4, 8, 1024, 4096], P('path', None, 'fsdp')
All inputs are finite; a program needn't handle non-finite values.
Results may differ from a plain program's by a relative error of at most 0.0024.
Values may be sent and summed in bfloat16 or wider, within the bound.
A program may use at most 320 MiB of HBM per device.

v0:
```python
import jax
import jax.numpy as jnp
from jax import lax
from jax.sharding import PartitionSpec as P

UNIT = 1024
SETS = 8
STEP = 1000
BETA_ONE = 0.9
BETA_TWO = 0.999
ADAM_EPS = 1e-08
INNER_RATE = 0.05
DECAY = 0.1
GLOBAL_LEARNING = 0.7
INERTIA_FACTOR = 0.9


def adam_delta(grads, first, second, start):
    corr_one = 1.0 - BETA_ONE**STEP
    corr_two = 1.0 - BETA_TWO**STEP
    first_new = BETA_ONE * first.astype(jnp.float32) + (1.0 - BETA_ONE) * grads
    second_new = BETA_TWO * second.astype(jnp.float32) + (1.0 - BETA_TWO) * grads * grads
    direction = first_new / corr_one / (jnp.sqrt(second_new / corr_two) + ADAM_EPS)
    return (INNER_RATE * (direction + DECAY * start.astype(jnp.float32))).astype(jnp.bfloat16)


def per_device(
    input_activation_matrix,
    output_sensitivity,
    trajectory_initial_parameters,
    trajectory_gradient_average,
    trajectory_squared_average,
    common_expert_parameters,
    outer_inertia,
    trajectory_membership,
    punctual_flags,
):
    set_count = trajectory_initial_parameters.shape[1]
    local_units = trajectory_initial_parameters.shape[2]
    row_width = trajectory_initial_parameters.shape[3]
    features = row_width // 2
    unit_rows = trajectory_initial_parameters[0].reshape(set_count * local_units, row_width)
    in_rows = unit_rows[:, :features]
    out_rows = unit_rows[:, features:]
    input_scale = features ** (-0.5)
    hidden_scale = (SETS * UNIT) ** (-0.5)
    contract_last = (((1,), (1,)), ((), ()))
    contract_first = (((0,), (0,)), ((), ()))
    inputs = lax.all_gather(input_activation_matrix[0], "fsdp", axis=0, tiled=True)
    upstream = lax.all_gather(output_sensitivity[0], "fsdp", axis=0, tiled=True)
    preact = (
        lax.dot_general(inputs, in_rows, contract_last, preferred_element_type=jnp.float32)
        * input_scale
    )
    active, pullback = jax.vjp(jax.nn.gelu, preact)
    active_half = active.astype(jnp.bfloat16)
    back_active = (
        lax.dot_general(upstream, out_rows, contract_last, preferred_element_type=jnp.float32)
        * hidden_scale
    )
    back_preact = pullback(back_active)[0].astype(jnp.bfloat16)
    grad_in = (
        lax.dot_general(back_preact, inputs, contract_first, preferred_element_type=jnp.float32)
        * input_scale
    )
    grad_out = (
        lax.dot_general(active_half, upstream, contract_first, preferred_element_type=jnp.float32)
        * hidden_scale
    )
    grad_in, grad_out = (grad_in, grad_out)
    grads = jnp.concatenate([grad_in, grad_out], axis=1)
    first_rows = trajectory_gradient_average[0].reshape(set_count * local_units, row_width)
    second_rows = trajectory_squared_average[0].reshape(set_count * local_units, row_width)
    pseudo = adam_delta(grads, first_rows, second_rows, unit_rows).reshape(
        set_count, local_units, row_width
    )
    path_count = lax.axis_size("path")
    position = lax.axis_index("path")
    owned_sets = set_count // path_count
    choices = common_expert_parameters.shape[1]
    eligible_trajectories = jnp.arange(choices, dtype=jnp.int32)
    picked_trajectories = jnp.where(
        (trajectory_membership[:, :, None] == eligible_trajectories[None, None, :])
        & (punctual_flags[:, None, None] == 1),
        1.0,
        0.0,
    ).astype(jnp.float32)
    first_set = position * owned_sets
    owner_module_weights = lax.dynamic_slice_in_dim(picked_trajectories, first_set, owned_sets, 1)
    punctual_tally = jnp.sum(owner_module_weights, axis=0)
    own_weights = lax.dynamic_index_in_dim(picked_trajectories, position, 0, keepdims=False)
    contributions = own_weights[:, :, None, None] * pseudo.astype(jnp.float32)[:, None]
    aggregate_change = lax.psum_scatter(
        contributions.astype(jnp.bfloat16), "path", scatter_dimension=0, tiled=True
    ).astype(jnp.float32)
    punctual_average = aggregate_change / jnp.maximum(punctual_tally, 1.0)[:, :, None, None]
    refreshed_inertia = INERTIA_FACTOR * outer_inertia + punctual_average
    refreshed_experts = common_expert_parameters - GLOBAL_LEARNING * (
        punctual_average + INERTIA_FACTOR * refreshed_inertia
    )
    updated = refreshed_experts.astype(jnp.bfloat16)
    all_modules = lax.all_gather(updated, "path", axis=0, tiled=True)
    own_choice = lax.dynamic_index_in_dim(trajectory_membership, position, 0, keepdims=False)
    returned = jnp.take_along_axis(all_modules, own_choice[:, None, None, None], axis=1)[:, 0]
    return (refreshed_experts, refreshed_inertia, returned[None])


def solution(mesh):
    placed = (
        P("path", "fsdp", None),
        P("path", "fsdp", None),
        P("path", None, "fsdp", None),
        P("path", None, "fsdp", None),
        P("path", None, "fsdp", None),
        P("path", None, "fsdp", None),
        P("path", None, "fsdp", None),
        P(),
        P(),
    )
    return jax.shard_map(
        per_device,
        mesh=mesh,
        in_specs=placed,
        out_specs=(
            P("path", None, "fsdp", None),
            P("path", None, "fsdp", None),
            P("path", None, "fsdp", None),
        ),
        check_vma=False,
    )
```

profile of v0, /device:TPU:0, one launch (start us, length us, event | category | flops | bytes accessed | tf_op | source)
XLA Modules:
  0.0 543.5 jit_solution(6791174297192927239)
XLA Ops:
  7.2 0.0 all-gather.10.cloned.1.call-start
  7.2 0.7 all-gather.10.cloned.1.call-update
  7.9 0.0 all-gather.8.cloned.1.call-start
  7.9 0.7 all-gather.8.cloned.1.call-update
  8.6 0.0 reduce-scatter.2.cloned.1.call-start
  8.7 0.7 broadcast_compare_fusion
  9.4 0.8 and_select_fusion
  10.1 0.1 copy.13
  10.2 101.4 %all-gather.10.cloned.1.call-done = bf16[1,1536,2048]{2,1,0:T(8,128)(2,1)} async-done(((bf16[1,192,2048]{2,1,0:T(8,128)(2,1)}), bf16[1,1536,2048]{2,1,0:T(8,128)(2,1)}) %all-gather.10.cloned.1.call-update) | async-done | bytes 6291472 | tf_op jit(solution)/shard_map/all_gather | solution.py:49
  111.6 11.7 %fusion.16 = f32[1536,1024]{1,0:T(8,128)} fusion(bf16[1,1536,2048]{2,1,0:T(8,128)(2,1)} %all-gather.10.cloned.1.call-done, bf16[1024,4096]{1,0:T(8,128)(2,1)} %bitcast.53), kind=kOutput, calls=%fused_computation.28 | convolution fusion | flops 6442450944 | bytes 16777216 | tf_op jit(solution)/shard_map/dot_general | solution.py:52
  123.3 87.4 %all-gather.8.cloned.1.call-done = bf16[1,1536,2048]{2,1,0:T(8,128)(2,1)} async-done(((bf16[1,192,2048]{2,1,0:T(8,128)(2,1)}), bf16[1,1536,2048]{2,1,0:T(8,128)(2,1)}) %all-gather.8.cloned.1.call-update) | async-done | bytes 6291472 | tf_op jit(solution)/shard_map/all_gather | solution.py:50
  210.7 26.1 %fusion.27 = f32[1024,2048]{1,0:T(8,128)} fusion(bf16[1,1536,2048]{2,1,0:T(8,128)(2,1)} %all-gather.10.cloned.1.call-done, f32[1536,1024]{1,0:T(8,128)} %fusion.16, bf16[1,1536,2048]{2,1,0:T(8,128)(2,1)} %all-gather.8.cloned.1.call-done, bf16[1024,4096]{1,0:T(8,128)(2,1)} %bitcast.54), kind=kOutput, calls=%fused_computation.36 | convolution fusion | flops 12921602048 | bytes 31457280 | tf_op jit(solution)/shard_map/dot_general | solution.py:63
  236.8 13.7 %fusion.24 = f32[1024,2048]{1,0:T(8,128)} fusion(bf16[1,1536,2048]{2,1,0:T(8,128)(2,1)} %all-gather.8.cloned.1.call-done, f32[1536,1024]{1,0:T(8,128)} %fusion.16), kind=kOutput, calls=%fused_computation.35 | convolution fusion | flops 6460276736 | bytes 20971520 | tf_op jit(solution)/shard_map/dot_general | solution.py:67
  250.4 18.0 %fusion.6 = f32[8,128,4096]{2,1,0:T(8,128)S(1)} fusion(bf16[1,8,128,4096]{3,2,1,0:T(8,128)(2,1)} %param.11, bf16[1,8,128,4096]{3,2,1,0:T(8,128)(2,1)} %param.13, f32[8,128,2048]{2,1,0:T(8,128)} %bitcast.56, f32[8,128,2048]{2,1,0:T(8,128)} %bitcast.55, bf16[1,8,128,4096]{3,2,1,0:T(8,128)(2,1)} %param.12), kind=kLoop, calls=%fused_computation.18 | loop fusion | flops 79691776 | bytes 58720256 | tf_op jit(solution)/shard_map/convert_element_type | solution.py:92
  268.5 7.6 %multiply_convert_fusion = bf16[8,2,128,4096]{3,2,1,0:T(8,128)(2,1)} fusion(f32[8,128,4096]{2,1,0:T(8,128)S(1)} %fusion.6, f32[8,2]{1,0:T(8,128)S(1)} %copy.13), kind=kLoop, calls=%fused_computation.1 | loop fusion | flops 16777216 | bytes 33554496 | tf_op jit(solution)/shard_map/convert_element_type | solution.py:94
  276.1 0.0 reduce-scatter.2.cloned.1.call-update
  276.1 0.0 all-gather.6.cloned.1.call-start
  276.2 0.1 dynamic-slice_reduce_fusion
  276.3 0.1 copy.14
  276.4 0.0 copy-start
  276.4 123.2 %reduce-scatter.2.cloned.1.call-done = bf16[2,2,128,4096]{3,2,1,0:T(8,128)(2,1)} async-done(((bf16[8,2,128,4096]{3,2,1,0:T(8,128)(2,1)}), bf16[2,2,128,4096]{3,2,1,0:T(8,128)(2,1)}) %reduce-scatter.2.cloned.1.call-update) | async-done | bytes 4194320 | tf_op jit(solution)/shard_map/reduce_scatter | solution.py:93
  399.5 13.0 %fusion.62 = (bf16[2,2,128,4096]{3,2,1,0:T(8,128)(2,1)}, f32[2,2,128,4096]{3,2,1,0:T(8,128)}, f32[2,2,128,4096]{3,2,1,0:T(8,128)}) fusion(f32[2,2,128,4096]{3,2,1,0:T(8,128)} %param.14, f32[2,2]{1,0:T(2,128)S(1)} %copy.14, bf16[2,2,128,4096]{3,2,1,0:T(8,128)(2,1)} %reduce-scatter.2.cloned.1.call-done, f32[2,2,128,4096]{3,2,1,0:T(8,128)} %param.15), kind=kLoop, calls=%fused_computation.76 | loop fusion | flops 18874368 | bytes 41943056 | tf_op jit(solution)/shard_map/convert_element_type | solution.py:101
  412.6 0.0 all-gather.6.cloned.1.call-update
  412.6 0.0 copy-done
  412.7 106.0 %all-gather.6.cloned.1.call-done = bf16[8,2,128,4096]{3,2,1,0:T(8,128)(2,1)} async-done(((bf16[2,2,128,4096]{3,2,1,0:T(8,128)(2,1)}), bf16[8,2,128,4096]{3,2,1,0:T(8,128)(2,1)}) %all-gather.6.cloned.1.call-update) | async-done | bytes 16777232 | tf_op jit(solution)/shard_map/all_gather | solution.py:102
  518.6 10.7 %gather_fusion = bf16[8,128,4096]{2,1,0:T(8,128)(2,1)} fusion(bf16[8,2,128,4096]{3,2,1,0:T(8,128)(2,1)} %all-gather.6.cloned.1.call-done, s32[8]{0:T(128)S(1)} %or_bitcast_fusion), kind=kCustom, calls=%fused_computation | custom fusion | bytes 16777280 | tf_op jit(solution)/shard_map/jit(take_along_axis)/gather | solution.py:104
  529.3 7.6 %bitcast_select_fusion = bf16[1,8,128,4096]{3,2,1,0:T(8,128)(2,1)} fusion(bf16[8,128,4096]{2,1,0:T(8,128)(2,1)} %gather_fusion, pred[8]{0:T(512)(128)(4,1)S(1)} %compare_and_fusion), kind=kLoop, calls=%fused_computation.14 | loop fusion | flops 4194304 | bytes 16777224 | tf_op jit(solution)/shard_map/jit(take_along_axis)/select_n | solution.py:104
  (7 shorter events, 0.1 us)
Async XLA Ops:
  7.2 104.4 %all-gather.10.cloned.1.call-start = ((), (), s32[]{:S(2)}) async-start(), calls=%async_computation.4 | async-start | bytes 7077888 | tf_op jit(solution)/shard_map/all_gather | solution.py:49
  7.9 202.8 %all-gather.8.cloned.1.call-start = ((), (), s32[]{:S(2)}) async-start(), calls=%async_computation.3 | async-start | bytes 7077888 | tf_op jit(solution)/shard_map/all_gather | solution.py:50
  8.6 390.9 %reduce-scatter.2.cloned.1.call-start = ((), (), s32[]{:S(2)}) async-start(), calls=%async_computation.1 | async-start | bytes 20971520 | tf_op jit(solution)/shard_map/reduce_scatter | solution.py:93
  276.1 242.5 %all-gather.6.cloned.1.call-start = ((), (), s32[]{:S(2)}) async-start(), calls=%async_computation.2 | async-start | bytes 20971520 | tf_op jit(solution)/shard_map/all_gather | solution.py:102
  276.4 136.2 %copy-start = (s32[4,8]{1,0:T(4,128)S(1)}, s32[4,8]{1,0:T(4,128)}, u32[]{:S(2)}) copy-start(s32[4,8]{1,0:T(4,128)} %param.16) | copy-start | bytes 388
Sparse Core Ops, SparseCore 0:
  10.2 101.3 all-gather.9
  113.8 96.8 all-gather.7
  276.3 123.2 reduce-scatter.1
  412.7 105.8 all-gather.5
where the time goes:
time: 544 us; the launch traced here: 543 us
  waiting for transfers between devices  419 us (77%)
  matrix products  51.5 us (9%)
  other arithmetic  47.9 us (9%)
  between operations  13.8 us (3%)
  local copies, waits for them, and re-layouts  10.8 us (2%)
    reduce_scatter x1, waiting for transfers between devices, per_device(): lax.psum_scatter(contributions.astype(jnp.bfloat16), 'path', scatter_dime...  123 us
    all_gather x1, waiting for transfers between devices, per_device(): all_modules = lax.all_gather(updated, 'path', axis=0, tiled=True)  106 us
    all_gather x1, waiting for transfers between devices, per_device(): lax.all_gather(input_activation_matrix[0], 'fsdp', axis=0, tiled=True)  101 us
    all_gather x1, waiting for transfers between devices, per_device(): upstream = lax.all_gather(output_sensitivity[0], 'fsdp', axis=0, tiled=True)  87.4 us
    dot_general x1, matrix products, per_device(): lax.dot_general(back_preact, inputs, contract_first, preferred_element_ty...  26.1 us
    convert_element_type x1, other arithmetic, per_device(): pseudo.astype(jnp.float32)[:, None]  18 us
    dot_general x1, matrix products, per_device(): lax.dot_general(active_half, upstream, contract_first, preferred_element_...  13.7 us
    convert_element_type x1, other arithmetic, per_device(): updated = refreshed_experts.astype(jnp.bfloat16)  13 us
  transfers between devices with their start and end apart: 4, of which 4 were waited for; matrix products, arithmetic and copies ran while one was open for 2% of the time, Pallas kernels for 0%

commit v1 on v0

--- a/solution.py
+++ b/solution.py
@@ -47,7 +47,10 @@
     contract_last = (((1,), (1,)), ((), ()))
     contract_first = (((0,), (0,)), ((), ()))
     inputs = lax.all_gather(input_activation_matrix[0], "fsdp", axis=0, tiled=True)
-    upstream = lax.all_gather(output_sensitivity[0], "fsdp", axis=0, tiled=True)
+    upstream = jnp.concatenate(
+        lax.all_to_all(jnp.stack([output_sensitivity[0]] * lax.axis_size("fsdp")), "fsdp", 0, 0),
+        axis=0,
+    )
     preact = (
         lax.dot_general(inputs, in_rows, contract_last, preferred_element_type=jnp.float32)
         * input_scale

time: 544 us -> 572 us (1.051)
  waiting for transfers between devices: 419 us -> 437 us
  starting transfers between devices: 0.16 us -> 7.4 us
    all_gather x1, waiting for transfers between devices: 101 us -> 207 us  [per_device(): lax.all_gather(input_activation_matrix[0], 'fsdp', axis=0, tiled=True)]
    all_gather x1 -> x0, waiting for transfers between devices: 87.4 us -> none  [per_device(): upstream = lax.all_gather(output_sensitivity[0], 'fsdp', axis=0, tiled=True)]
    all_to_all x0 -> x1, starting transfers between devices: none -> 7.28 us  [per_device(): lax.all_to_all(jnp.stack([output_sensitivity[0]] * lax.axis_size('fsdp'))...]
  transfers between devices with their start and end apart: 4 -> 4, of which waited for: 4 -> 3; matrix products, arithmetic and copies ran while one was open for 2% -> 3% of each run, Pallas kernels for 0% -> 0%
where the time goes in v1:
time: 572 us
  waiting for transfers between devices  437 us (76%)
  matrix products  51.5 us (9%)
  other arithmetic  46.8 us (8%)
  local copies, waits for them, and re-layouts  15.5 us (3%)
  between operations  13.8 us (2%)
  starting transfers between devices  7.4 us (1%)
    all_gather x1, waiting for transfers between devices, per_device(): lax.all_gather(input_activation_matrix[0], 'fsdp', axis=0, tiled=True)  207 us
    reduce_scatter x1, waiting for transfers between devices, per_device(): lax.psum_scatter(contributions.astype(jnp.bfloat16), 'path', scatter_dime...  123 us
    all_gather x1, waiting for transfers between devices, per_device(): all_modules = lax.all_gather(updated, 'path', axis=0, tiled=True)  106 us
    dot_general x1, matrix products, per_device(): lax.dot_general(back_preact, inputs, contract_first, preferred_element_ty...  26.1 us
    convert_element_type x1, other arithmetic, per_device(): pseudo.astype(jnp.float32)[:, None]  18 us
    dot_general x1, matrix products, per_device(): lax.dot_general(active_half, upstream, contract_first, preferred_element_...  13.7 us
    convert_element_type x1, other arithmetic, per_device(): updated = refreshed_experts.astype(jnp.bfloat16)  13 us
    dot_general x1, matrix products, per_device(): lax.dot_general(inputs, in_rows, contract_last, preferred_element_type=jn...  11.7 us
  transfers between devices with their start and end apart: 4, of which 3 were waited for; matrix products, arithmetic and copies ran while one was open for 3% of the time, Pallas kernels for 0%

profile of v1, /device:TPU:0, one launch (start us, length us, event | category | flops | bytes accessed | tf_op | source)
XLA Modules:
  0.0 571.6 jit_solution(6753261386714020467)
XLA Ops:
  7.2 0.0 all-gather.6.cloned.1.call-start
  7.2 0.7 all-gather.6.cloned.1.call-update
  7.9 0.0 copy-start.1
  7.9 0.0 copy-start
  7.9 4.6 stack.3
  12.6 7.3 %all-to-all-start = ((bf16[8,192,2048]{2,1,0:T(8,128)(2,1)}), bf16[8,192,2048]{2,1,0:T(8,128)(2,1)}, u32[]{:S(2)}, u32[]{:S(2)}) async-start(bf16[8,192,2048]{2,1,0:T(8,128)(2,1)} %stack.3), calls=%async_computation | async-start | bytes 12582912 | tf_op jit(solution)/shard_map/all_to_all | solution.py:51
  19.8 0.0 reduce-scatter.2.cloned.1.call-start
  19.9 0.0 copy-done.1
  19.9 0.0 copy-done
  19.9 0.1 and_select_fusion
  20.0 0.1 copy.13
  20.1 206.9 %all-gather.6.cloned.1.call-done = bf16[1,1536,2048]{2,1,0:T(8,128)(2,1)} async-done(((bf16[1,192,2048]{2,1,0:T(8,128)(2,1)}), bf16[1,1536,2048]{2,1,0:T(8,128)(2,1)}) %all-gather.6.cloned.1.call-update) | async-done | bytes 6291472 | tf_op jit(solution)/shard_map/all_gather | solution.py:49
  227.0 11.7 %fusion.16 = f32[1536,1024]{1,0:T(8,128)} fusion(bf16[1,1536,2048]{2,1,0:T(8,128)(2,1)} %all-gather.6.cloned.1.call-done, bf16[1024,4096]{1,0:T(8,128)(2,1)} %bitcast.46), kind=kOutput, calls=%fused_computation.28 | convolution fusion | flops 6442450944 | bytes 16777216 | tf_op jit(solution)/shard_map/dot_general | solution.py:55
  238.7 0.0 all-to-all-done
  238.7 13.7 %convolution_multiply_fusion = f32[1024,2048]{1,0:T(8,128)} fusion(bf16[1536,2048]{1,0:T(8,128)(2,1)} %bitcast.3, f32[1536,1024]{1,0:T(8,128)} %fusion.16), kind=kOutput, calls=%fused_computation.32 | convolution fusion | flops 6460276736 | bytes 20971520 | tf_op jit(solution)/shard_map/dot_general | solution.py:70
  252.4 26.1 %fusion.18 = f32[1024,2048]{1,0:T(8,128)} fusion(bf16[1,1536,2048]{2,1,0:T(8,128)(2,1)} %all-gather.6.cloned.1.call-done, f32[1536,1024]{1,0:T(8,128)} %fusion.16, bf16[1536,2048]{1,0:T(8,128)(2,1)} %bitcast.3, bf16[1024,4096]{1,0:T(8,128)(2,1)} %bitcast.47), kind=kOutput, calls=%fused_computation.31 | convolution fusion | flops 12921602048 | bytes 31457280 | tf_op jit(solution)/shard_map/dot_general | solution.py:66
  278.5 18.0 %fusion.6 = f32[8,128,4096]{2,1,0:T(8,128)S(1)} fusion(bf16[1,8,128,4096]{3,2,1,0:T(8,128)(2,1)} %param.11, bf16[1,8,128,4096]{3,2,1,0:T(8,128)(2,1)} %param.13, f32[8,128,2048]{2,1,0:T(8,128)} %bitcast.48, f32[8,128,2048]{2,1,0:T(8,128)} %bitcast.49, bf16[1,8,128,4096]{3,2,1,0:T(8,128)(2,1)} %param.12), kind=kLoop, calls=%fused_computation.18 | loop fusion | flops 79691776 | bytes 58720256 | tf_op jit(solution)/shard_map/convert_element_type | solution.py:95
  296.6 7.8 %multiply_convert_fusion = bf16[8,2,128,4096]{3,2,1,0:T(8,128)(2,1)} fusion(f32[8,128,4096]{2,1,0:T(8,128)S(1)} %fusion.6, f32[8,2]{1,0:T(8,128)S(1)} %copy.13), kind=kLoop, calls=%fused_computation.1 | loop fusion | flops 16777216 | bytes 33554496 | tf_op jit(solution)/shard_map/convert_element_type | solution.py:97
  304.4 0.0 reduce-scatter.2.cloned.1.call-update
  304.4 0.0 all-gather.4.cloned.1.call-start
  304.5 0.1 dynamic-slice_reduce_fusion
  304.6 0.1 copy.14
  304.7 123.0 %reduce-scatter.2.cloned.1.call-done = bf16[2,2,128,4096]{3,2,1,0:T(8,128)(2,1)} async-done(((bf16[8,2,128,4096]{3,2,1,0:T(8,128)(2,1)}), bf16[2,2,128,4096]{3,2,1,0:T(8,128)(2,1)}) %reduce-scatter.2.cloned.1.call-update) | async-done | bytes 4194320 | tf_op jit(solution)/shard_map/reduce_scatter | solution.py:96
  427.7 13.0 %fusion.51 = (bf16[2,2,128,4096]{3,2,1,0:T(8,128)(2,1)}, f32[2,2,128,4096]{3,2,1,0:T(8,128)}, f32[2,2,128,4096]{3,2,1,0:T(8,128)}) fusion(f32[2,2,128,4096]{3,2,1,0:T(8,128)} %param.14, f32[2,2]{1,0:T(2,128)S(1)} %copy.14, bf16[2,2,128,4096]{3,2,1,0:T(8,128)(2,1)} %reduce-scatter.2.cloned.1.call-done, f32[2,2,128,4096]{3,2,1,0:T(8,128)} %param.15), kind=kLoop, calls=%fused_computation.72 | loop fusion | flops 18874368 | bytes 41943056 | tf_op jit(solution)/shard_map/convert_element_type | solution.py:104
  440.7 0.0 all-gather.4.cloned.1.call-update
  440.8 106.0 %all-gather.4.cloned.1.call-done = bf16[8,2,128,4096]{3,2,1,0:T(8,128)(2,1)} async-done(((bf16[2,2,128,4096]{3,2,1,0:T(8,128)(2,1)}), bf16[8,2,128,4096]{3,2,1,0:T(8,128)(2,1)}) %all-gather.4.cloned.1.call-update) | async-done | bytes 16777232 | tf_op jit(solution)/shard_map/all_gather | solution.py:105
  546.8 10.7 %gather_fusion = bf16[8,128,4096]{2,1,0:T(8,128)(2,1)} fusion(bf16[8,2,128,4096]{3,2,1,0:T(8,128)(2,1)} %all-gather.4.cloned.1.call-done, s32[8]{0:T(128)S(1)} %or_bitcast_fusion), kind=kCustom, calls=%fused_computation | custom fusion | bytes 16777280 | tf_op jit(solution)/shard_map/jit(take_along_axis)/gather | solution.py:107
  557.4 7.6 %bitcast_select_fusion = bf16[1,8,128,4096]{3,2,1,0:T(8,128)(2,1)} fusion(bf16[8,128,4096]{2,1,0:T(8,128)(2,1)} %gather_fusion, pred[8]{0:T(512)(128)(4,1)S(1)} %compare_and_fusion), kind=kLoop, calls=%fused_computation.14 | loop fusion | flops 4194304 | bytes 16777224 | tf_op jit(solution)/shard_map/jit(take_along_axis)/select_n | solution.py:107
  (8 shorter events, 0.1 us)
Async XLA Ops:
  7.2 219.9 %all-gather.6.cloned.1.call-start = ((), (), s32[]{:S(2)}) async-start(), calls=%async_computation.4 | async-start | bytes 7077888 | tf_op jit(solution)/shard_map/all_gather | solution.py:49
  7.9 12.0 %copy-start.1 = (s32[4]{0:T(128)S(1)}, s32[4]{0:T(128)}, u32[]{:S(2)}) copy-start(s32[4]{0:T(128)} %param.17) | copy-start | bytes 52
  7.9 12.0 %copy-start = (s32[4,8]{1,0:T(4,128)S(1)}, s32[4,8]{1,0:T(4,128)}, u32[]{:S(2)}) copy-start(s32[4,8]{1,0:T(4,128)} %param.16) | copy-start | bytes 388
  12.6 226.2 %all-to-all-start = ((bf16[8,192,2048]{2,1,0:T(8,128)(2,1)}), bf16[8,192,2048]{2,1,0:T(8,128)(2,1)}, u32[]{:S(2)}, u32[]{:S(2)}) async-start(bf16[8,192,2048]{2,1,0:T(8,128)(2,1)} %stack.3), calls=%async_computation | async-start | bytes 12582912 | tf_op jit(solution)/shard_map/all_to_all | solution.py:51
  19.8 407.8 %reduce-scatter.2.cloned.1.call-start = ((), (), s32[]{:S(2)}) async-start(), calls=%async_computation.2 | async-start | bytes 20971520 | tf_op jit(solution)/shard_map/reduce_scatter | solution.py:96
  304.4 242.4 %all-gather.4.cloned.1.call-start = ((), (), s32[]{:S(2)}) async-start(), calls=%async_computation.3 | async-start | bytes 20971520 | tf_op jit(solution)/shard_map/all_gather | solution.py:105
Sparse Core Ops, SparseCore 0:
  10.2 216.8 all-gather.5
  304.5 123.0 reduce-scatter.1
  440.8 105.8 all-gather.3
